TPU v7x, 32 devices: a whole 2x2x4 slice. The times are simulated.
32 devices in a mesh: batch: 8 (over z, y), vocab: 4 (over x, core).
Axes of the slice: x: 2, y: 2, z: 4, core: 2. Of those that a mesh axis runs over, the one named last changes fastest.
Arguments:
- hidden: bfloat16 [4096, 3584], P(('batch', 'vocab')), may hold values from -6 to 6
- head_weight: bfloat16 [3072, 3584], P('vocab', 'batch'), may hold values from -0.3125 to 0.3125
- targets: int32 [4096], P(('batch', 'vocab')), may hold values from 0 to 3071
- valid_mask: int32 [4096], P(('batch', 'vocab')), may hold values 0 or 1
Outputs:
- head_grad: float32 [3072, 3584], P('vocab', 'batch')
- hidden_grad: float32 [4096, 3584], P(('batch', 'vocab'))
- mean_loss: float32 [], replicated
All inputs are finite; a program needn't handle non-finite values. No bound on the sum of `valid_mask` on one device may be relied on, other than what follows from the above.
Results may differ from a plain program's by a relative error of at most 0.0019.
Values may be sent and summed in bfloat16 or wider, within the bound.
A program may use at most 128 MiB of HBM per device.

v0:
```python
import jax
import jax.numpy as jnp
from jax import lax
from jax.sharding import PartitionSpec as P

softcap = 30.0


def capped(scores):
    return softcap * jnp.tanh(scores / softcap)


def local(hidden, head_weight, targets, valid_mask):
    own_rows = head_weight.shape[0]
    batch_count = lax.axis_size("batch")
    vocab_index = lax.axis_index("vocab")
    group_ids, group_mask = (
        lax.all_gather(targets, "vocab", axis=0, tiled=True),
        lax.all_gather(valid_mask, "vocab", axis=0, tiled=True),
    )
    group_states = lax.all_gather(hidden, "vocab", axis=0, tiled=True)
    group_tokens = group_states.shape[0]
    first_row = vocab_index * own_rows
    inside = (group_ids >= first_row) & (group_ids < first_row + own_rows)
    local_index = jnp.where(inside, group_ids - first_row, -1)
    columns = jnp.arange(own_rows, dtype=jnp.int32)
    weight = group_mask.astype(jnp.float32)
    state_cols = group_states
    scores = lax.dot_general(
        state_cols,
        lax.all_gather(head_weight, "batch", axis=1, tiled=True),
        (((1,), (1,)), ((), ())),
        preferred_element_type=jnp.float32,
    )
    logits = capped(scores)
    target_hit = columns[None, :] == local_index[:, None]
    exponent = jnp.exp(logits)
    partition, target_logit = lax.psum(
        (jnp.sum(exponent, axis=1), jnp.sum(jnp.where(target_hit, logits, 0.0), axis=1)), "vocab"
    )
    slope = 1.0 - (logits / softcap) ** 2
    delta_logit = (
        weight[:, None] * (exponent / partition[:, None] - target_hit.astype(jnp.float32)) * slope
    ).astype(jnp.bfloat16)
    state_cols = group_states
    grad_columns = lax.psum_scatter(
        lax.dot_general(
            state_cols, delta_logit, (((0,), (0,)), ((), ())), preferred_element_type=jnp.float32
        ),
        "batch",
        scatter_dimension=0,
        tiled=True,
    )
    head_grad = jnp.transpose(grad_columns)
    partial_grad = jnp.dot(
        delta_logit,
        lax.all_gather(head_weight, "batch", axis=1, tiled=True),
        preferred_element_type=jnp.float32,
    )
    hidden_grad = lax.psum_scatter(partial_grad, "vocab", scatter_dimension=0, tiled=True)
    token_loss = weight * (jnp.log(partition) - target_logit)
    total_tokens = group_tokens * batch_count
    loss_total = lax.psum(jnp.sum(token_loss), "batch")
    mean_loss = loss_total / total_tokens
    return (head_grad, hidden_grad, mean_loss)


def solution(mesh):
    placed = (
        P(("batch", "vocab"), None),
        P("vocab", "batch"),
        P(("batch", "vocab")),
        P(("batch", "vocab")),
    )
    return jax.shard_map(
        local,
        mesh=mesh,
        in_specs=placed,
        out_specs=(P("vocab", "batch"), P(("batch", "vocab"), None), P()),
        check_vma=False,
    )
```

profile of v0, /device:TPU:0, one launch (start us, length us, event | category | flops | bytes accessed | tf_op | source)
XLA Modules:
  0.0 417.8 jit_solution(7849890568541200374)
XLA Ops:
  7.2 0.0 copy-start
  7.2 0.0 copy-start.1
  7.2 0.0 all-gather.5.cloned.1.call-start
  7.2 0.7 all-gather.5.cloned.1.call-update
  7.9 0.0 all-gather.7.cloned.1.call-start
  8.0 0.7 all-gather.7.cloned.1.call-update
  8.7 0.0 reduce-scatter.5.cloned.1.call-start
  8.7 0.0 copy-done
  8.7 6.0 %all-gather = s32[4,1,128]{2,1,0:T(1,128)S(1)} all-gather(s32[1,1,128]{2,1,0:T(1,128)S(1)} %bitcast.19), channel_id=1, replica_groups=mesh['batch'=8,'vocab'=4] {'vocab'}, dimensions={0}, use_global_device_ids=true | all-gather | bytes 2560 | tf_op jit(solution)/shard_map/all_gather | solution.py:19
  14.7 0.0 copy-done.1
  14.7 5.4 %all-gather.1 = s32[4,1,128]{2,1,0:T(1,128)S(1)} all-gather(s32[1,1,128]{2,1,0:T(1,128)S(1)} %bitcast.20), channel_id=1, replica_groups=mesh['batch'=8,'vocab'=4] {'vocab'}, dimensions={0}, use_global_device_ids=true | all-gather | bytes 2560 | tf_op jit(solution)/shard_map/all_gather | solution.py:18
  20.1 23.7 %all-gather.5.cloned.1.call-done = bf16[512,3584]{1,0:T(8,128)(2,1)} async-done(((bf16[128,3584]{1,0:T(8,128)(2,1)}), bf16[512,3584]{1,0:T(8,128)(2,1)}) %all-gather.5.cloned.1.call-update) | async-done | bytes 3670032 | tf_op jit(solution)/shard_map/all_gather | solution.py:21
  43.8 91.3 %all-gather.7.cloned.1.call-done = bf16[768,3584]{0,1:T(8,128)(2,1)} async-done(((bf16[768,448]{0,1:T(8,128)(2,1)}), bf16[768,3584]{0,1:T(8,128)(2,1)}) %all-gather.7.cloned.1.call-update) | async-done | bytes 5505040 | tf_op jit(solution)/shard_map/all_gather | solution.py:31
  135.1 7.0 %select_reduce_fusion = (f32[512]{0:T(512)S(1)}, f32[512]{0:T(512)S(1)}, f32[512,768]{1,0:T(8,128)S(1)}) fusion(s32[512]{0:T(512)S(1)} %bitcast.16, bf16[512,3584]{1,0:T(8,128)(2,1)} %all-gather.5.cloned.1.call-done, bf16[768,3584]{0,1:T(8,128)(2,1)} %all-gather.7.cloned.1.call-done), kind=kOutput, calls=%fused_computation.1 | convolution fusion | flops 2820930560 | bytes 10754048 | tf_op jit(solution)/shard_map/dot_general | solution.py:29
  142.1 5.7 %all-reduce = (f32[512]{0:T(512)S(1)}, f32[512]{0:T(512)S(1)}) all-reduce(f32[512]{0:T(512)S(1)} %get-tuple-element.10, f32[512]{0:T(512)S(1)} %get-tuple-element.9), channel_id=1, replica_groups=mesh['batch'=8,'vocab'=4] {'vocab'}, use_global_device_ids=true, to_apply=%region_1.2 | all-reduce | flops 1024 | bytes 8192 | tf_op jit(solution)/shard_map/psum | solution.py:38
  147.8 8.2 %fusion = f32[512,3584]{1,0:T(8,128)} fusion(bf16[768,3584]{0,1:T(8,128)(2,1)} %all-gather.7.cloned.1.call-done, f32[512,768]{1,0:T(8,128)S(1)} %get-tuple-element.13, s32[512]{0:T(512)S(1)} %bitcast.17, f32[512]{0:T(512)S(1)} %get-tuple-element.11, f32[512]{0:T(512)S(1)} %bitcast.13), kind=kOutput, calls=%fused_computation.8 | convolution fusion | flops 2822504448 | bytes 14424064 | tf_op jit(solution)/shard_map/dot_general | solution.py:55
  156.0 0.0 reduce-scatter.5.cloned.1.call-update
  156.0 0.0 reduce-scatter.7.cloned.1.call-start
  156.1 8.9 %convolution_bitcast_fusion = f32[3584,768]{0,1:T(8,128)} fusion(bf16[512,3584]{1,0:T(8,128)(2,1)} %all-gather.5.cloned.1.call-done, f32[512,768]{1,0:T(8,128)S(1)} %get-tuple-element.13, s32[512]{0:T(512)S(1)} %bitcast.18, f32[512]{0:T(512)S(1)} %get-tuple-element.11, f32[512]{0:T(512)S(1)} %bitcast.14), kind=kOutput, calls=%fused_computation | convolution fusion | flops 2822504448 | bytes 16259072 | tf_op jit(solution)/shard_map/dot_general | solution.py:47
  165.0 12.7 %copy.9 = f32[3584,768]{1,0:T(8,128)} copy(f32[3584,768]{0,1:T(8,128)} %convolution_bitcast_fusion) | data formatting | bytes 22020096
  177.7 0.0 reduce-scatter.7.cloned.1.call-update
  177.7 0.6 multiply_reduce_fusion
  178.3 19.4 %psum.23 = f32[]{:T(128)} all-reduce(f32[]{:T(128)} %multiply_reduce_fusion), channel_id=1, replica_groups=mesh['batch'=8,'vocab'=4] {'batch'}, use_global_device_ids=true, to_apply=%region_7.8 | all-reduce | flops 1 | bytes 8 | tf_op jit(solution)/shard_map/psum | solution.py:63
  198.4 22.1 %reduce-scatter.5.cloned.1.call-done = f32[128,3584]{1,0:T(8,128)} async-done(((f32[512,3584]{1,0:T(8,128)}), f32[128,3584]{1,0:T(8,128)}) %reduce-scatter.5.cloned.1.call-update) | async-done | bytes 1835024 | tf_op jit(solution)/shard_map/reduce_scatter | solution.py:60
  220.5 189.6 %reduce-scatter.7.cloned.1.call-done = f32[448,768]{1,0:T(8,128)} async-done(((f32[3584,768]{1,0:T(8,128)}), f32[448,768]{1,0:T(8,128)}) %reduce-scatter.7.cloned.1.call-update) | async-done | bytes 1376272
  (2 shorter events, 0.0 us)
Async XLA Ops:
  7.2 1.6 copy-start
  7.2 7.6 %copy-start.1 = (s32[128]{0:T(128)S(1)}, s32[128]{0:T(128)}, u32[]{:S(2)}) copy-start(s32[128]{0:T(128)} %param.6) | copy-start | bytes 1540
  7.2 36.6 %all-gather.5.cloned.1.call-start = ((), (), s32[]{:S(2)}) async-start(), calls=%async_computation.2 | async-start | bytes 4587520 | tf_op jit(solution)/shard_map/all_gather | solution.py:21
  7.9 127.2 %all-gather.7.cloned.1.call-start = ((), (), s32[]{:S(2)}) async-start(), calls=%async_computation.3 | async-start | bytes 6193152 | tf_op jit(solution)/shard_map/all_gather | solution.py:31
  8.7 211.9 %reduce-scatter.5.cloned.1.call-start = ((), (), s32[]{:S(2)}) async-start(), calls=%async_computation.4 | async-start | bytes 9175040 | tf_op jit(solution)/shard_map/reduce_scatter | solution.py:60
  156.0 254.1 %reduce-scatter.7.cloned.1.call-start = ((), (), s32[]{:S(2)}) async-start(), calls=%async_computation.5 | async-start | bytes 12386304
Sparse Core Ops, SparseCore 0:
  9.6 34.1 all-gather.4
  46.0 89.1 all-gather.6
  156.1 64.3 reduce-scatter.4
  224.6 185.4 reduce-scatter.6
where the time goes:
time: 418 us
  waiting for transfers between devices  328 us (78%)
  blocking collectives  36.5 us (9%)
  matrix products  24.1 us (6%)
  between operations  15.6 us (4%)
  local copies, waits for them, and re-layouts  12.7 us (3%)
    unnamed x5, waiting for transfers between devices  191 us
    all_gather x1, waiting for transfers between devices, local(): lax.all_gather(head_weight, 'batch', axis=1, tiled=True)  91.3 us
    all_gather x1, waiting for transfers between devices, local(): group_states = lax.all_gather(hidden, 'vocab', axis=0, tiled=True)  23.7 us
    reduce_scatter x1, waiting for transfers between devices, local(): lax.psum_scatter(partial_grad, 'vocab', scatter_dimension=0, tiled=True)  22.1 us
    psum x1, blocking collectives, local(): loss_total = lax.psum(jnp.sum(token_loss), 'batch')  19.4 us
    unnamed x5, local copies, waits for them, and re-layouts  12.7 us
    dot_general x1, matrix products, local(): lax.dot_general(state_cols, delta_logit, (((0,), (0,)), ((), ())), prefer...  8.94 us
  transfers between devices with their start and end apart: 4, of which 4 were waited for; matrix products, arithmetic and copies ran while one was open for 5% of the time, Pallas kernels for 0%

commit v1 on v0

--- a/solution.py
+++ b/solution.py
@@ -4,6 +4,16 @@
 from jax.sharding import PartitionSpec as P
 
 softcap = 30.0
+
+
+def turned_line(value, mesh_axis, d):
+    peers = lax.axis_size(mesh_axis)
+    held, blocks = (value, [value])
+    for _ in range(peers - 1):
+        held = lax.ppermute(held, mesh_axis, [(i, (i + 1) % peers) for i in range(peers)])
+        blocks.insert(0, held)
+    line = jnp.concatenate(blocks, axis=d)
+    return jnp.roll(line, (lax.axis_index(mesh_axis) + 1) * value.shape[d], axis=d)
 
 
 def capped(scores):
@@ -18,7 +28,7 @@
         lax.all_gather(targets, "vocab", axis=0, tiled=True),
         lax.all_gather(valid_mask, "vocab", axis=0, tiled=True),
     )
-    group_states = lax.all_gather(hidden, "vocab", axis=0, tiled=True)
+    group_states = turned_line(hidden, "vocab", 0)
     group_tokens = group_states.shape[0]
     first_row = vocab_index * own_rows
     inside = (group_ids >= first_row) & (group_ids < first_row + own_rows)

time: 418 us -> 386 us (0.923)
  waiting for transfers between devices: 328 us -> 289 us
  blocking collectives: 36.5 us -> 45.5 us
  local copies, waits for them, and re-layouts: 12.7 us -> 8.04 us
    unnamed x5 -> x3, waiting for transfers between devices: 191 us -> 0.71 us
    reduce_scatter x0 -> x1, waiting for transfers between devices: none -> 190 us  [local(): lax.psum_scatter(lax.dot_general(state_cols, delta_logit, (((0,), (0,)),...]
    all_gather x1, waiting for transfers between devices: 91.3 us -> 40.3 us  [local(): lax.all_gather(head_weight, 'batch', axis=1, tiled=True)]
    ppermute x0 -> x3, waiting for transfers between devices: none -> 26 us  [turned_line(): lax.ppermute(held, mesh_axis, [(i, (i + 1) % peers) for i in range(peers)])]
    all_gather x1 -> x0, waiting for transfers between devices: 23.7 us -> none  [local(): group_states = lax.all_gather(hidden, 'vocab', axis=0, tiled=True)]
    reduce_scatter x1, waiting for transfers between devices: 22.1 us -> 31.6 us  [local(): lax.psum_scatter(partial_grad, 'vocab', scatter_dimension=0, tiled=True)]
    all_gather x1, blocking collectives: 6.01 us -> 13.6 us  [local(): lax.all_gather(valid_mask, 'vocab', axis=0, tiled=True)]
    unnamed x5 -> x9, local copies, waits for them, and re-layouts: 12.7 us -> 6.95 us
  transfers between devices with their start and end apart: 4 -> 6, of which waited for: 4 -> 5; matrix products, arithmetic and copies ran while one was open for 5% -> 5% of each run, Pallas kernels for 0% -> 0%
where the time goes in v1:
time: 386 us; the launch traced here: 385 us
  waiting for transfers between devices  289 us (75%)
  blocking collectives  45.5 us (12%)
  matrix products  26.2 us (7%)
  between operations  15.5 us (4%)
  local copies, waits for them, and re-layouts  8.04 us (2%)
    reduce_scatter x1, waiting for transfers between devices, local(): lax.psum_scatter(lax.dot_general(state_cols, delta_logit, (((0,), (0,)),...  190 us
    all_gather x1, waiting for transfers between devices, local(): lax.all_gather(head_weight, 'batch', axis=1, tiled=True)  40.3 us
    reduce_scatter x1, waiting for transfers between devices, local(): lax.psum_scatter(partial_grad, 'vocab', scatter_dimension=0, tiled=True)  31.6 us
    ppermute x3, waiting for transfers between devices, turned_line(): lax.ppermute(held, mesh_axis, [(i, (i + 1) % peers) for i in range(peers)])  26 us
    psum x1, blocking collectives, local(): loss_total = lax.psum(jnp.sum(token_loss), 'batch')  20.6 us
    all_gather x1, blocking collectives, local(): lax.all_gather(valid_mask, 'vocab', axis=0, tiled=True)  13.6 us
    dot_general x1, matrix products, local(): lax.dot_general(state_cols, delta_logit, (((0,), (0,)), ((), ())), prefer...  11 us
    dot_general x1, matrix products, local(): jnp.dot(delta_logit, lax.all_gather(head_weight, 'batch', axis=1, tiled=T...  8.19 us
  transfers between devices with their start and end apart: 6, of which 5 were waited for; matrix products, arithmetic and copies ran while one was open for 5% of the time, Pallas kernels for 0%

profile of v1, /device:TPU:0, one launch (start us, length us, event | category | flops | bytes accessed | tf_op | source)
XLA Modules:
  0.0 385.3 jit_solution(4640610476716631942)
XLA Ops:
  7.2 0.0 all-gather.4.cloned.1.call-start
  7.2 0.7 all-gather.4.cloned.1.call-update
  7.9 0.0 reduce-scatter.5.cloned.1.call-start
  7.9 0.5 collective-permute-start
  8.5 13.2 %collective-permute-done = bf16[128,3584]{1,0:T(8,128)(2,1)S(1)} collective-permute-done((bf16[128,3584]{1,0:T(8,128)(2,1)}, bf16[128,3584]{1,0:T(8,128)(2,1)S(1)}, u32[]{:S(2)}, u32[]{:S(2)}) %collective-permute-start) | collective-permute-done | bytes 917536 | tf_op jit(solution)/shard_map/ppermute | solution.py:13
  21.7 0.0 collective-permute-start.1
  21.7 12.8 %collective-permute-done.1 = bf16[128,3584]{1,0:T(8,128)(2,1)S(1)} collective-permute-done((bf16[128,3584]{1,0:T(8,128)(2,1)S(1)}, bf16[128,3584]{1,0:T(8,128)(2,1)S(1)}, u32[]{:S(2)}, u32[]{:S(2)}) %collective-permute-start.1) | collective-permute-done | bytes 917536 | tf_op jit(solution)/shard_map/ppermute | solution.py:13
  34.5 0.0 collective-permute-start.2
  34.5 13.6 %all-gather = s32[4,1,128]{2,1,0:T(1,128)S(1)} all-gather(s32[1,1,128]{2,1,0:T(1,128)} %bitcast.13), channel_id=1, replica_groups=mesh['batch'=8,'vocab'=4] {'vocab'}, dimensions={0}, use_global_device_ids=true | all-gather | bytes 2560 | tf_op jit(solution)/shard_map/all_gather | solution.py:29
  48.2 5.6 %all-gather.1 = s32[4,1,128]{2,1,0:T(1,128)S(1)} all-gather(s32[1,1,128]{2,1,0:T(1,128)} %bitcast.14), channel_id=1, replica_groups=mesh['batch'=8,'vocab'=4] {'vocab'}, dimensions={0}, use_global_device_ids=true | all-gather | bytes 2560 | tf_op jit(solution)/shard_map/all_gather | solution.py:28
  53.7 0.0 collective-permute-done.2
  53.7 1.0 constant_dynamic-update-slice_fusion.7
  54.7 0.0 copy-start
  54.7 1.0 constant_dynamic-update-slice_fusion.6
  55.7 1.0 constant_dynamic-update-slice_fusion.5
  56.7 0.0 copy-done
  56.7 1.0 constant_dynamic-update-slice_fusion.4
  57.7 1.0 constant_dynamic-update-slice_fusion.3
  58.7 1.0 constant_dynamic-update-slice_fusion.2
  59.7 1.0 constant_dynamic-update-slice_fusion.1
  60.7 1.1 constant_dynamic-update-slice_fusion
  61.8 40.3 %all-gather.4.cloned.1.call-done = bf16[768,3584]{0,1:T(8,128)(2,1)} async-done(((bf16[768,448]{0,1:T(8,128)(2,1)}), bf16[768,3584]{0,1:T(8,128)(2,1)}) %all-gather.4.cloned.1.call-update) | async-done | bytes 5505040 | tf_op jit(solution)/shard_map/all_gather | solution.py:41
  102.0 7.0 %select_reduce_fusion = (f32[512]{0:T(512)S(1)}, f32[512]{0:T(512)S(1)}, f32[512,768]{1,0:T(8,128)S(1)}) fusion(s32[512]{0:T(512)S(1)} %bitcast.10, bf16[768,3584]{0,1:T(8,128)(2,1)} %all-gather.4.cloned.1.call-done, bf16[1024,3584]{1,0:T(8,128)(2,1)} %constant_dynamic-update-slice_fusion, s32[]{:T(128)S(6)} %select_n.22), kind=kOutput, calls=%fused_computation.4 | convolution fusion | flops 2820930560 | bytes 10754052 | tf_op jit(solution)/shard_map/dot_general | solution.py:39
  109.1 5.7 %all-reduce = (f32[512]{0:T(512)S(1)}, f32[512]{0:T(512)S(1)}) all-reduce(f32[512]{0:T(512)S(1)} %get-tuple-element.4, f32[512]{0:T(512)S(1)} %get-tuple-element.3), channel_id=1, replica_groups=mesh['batch'=8,'vocab'=4] {'vocab'}, use_global_device_ids=true, to_apply=%region_1.2 | all-reduce | flops 1024 | bytes 8192 | tf_op jit(solution)/shard_map/psum | solution.py:48
  114.7 8.2 %fusion.8 = f32[512,3584]{1,0:T(8,128)} fusion(bf16[768,3584]{0,1:T(8,128)(2,1)} %all-gather.4.cloned.1.call-done, f32[512,768]{1,0:T(8,128)S(1)} %get-tuple-element.7, s32[512]{0:T(512)S(1)} %bitcast.11, f32[512]{0:T(512)S(1)} %get-tuple-element.5, f32[512]{0:T(512)S(1)} %bitcast.7), kind=kOutput, calls=%fused_computation.21 | convolution fusion | flops 2822504448 | bytes 14424064 | tf_op jit(solution)/shard_map/dot_general | solution.py:65
  122.9 0.0 reduce-scatter.5.cloned.1.call-update
  122.9 0.0 reduce-scatter.3.cloned.1.call-start
  123.0 11.0 %fusion = f32[3584,768]{1,0:T(8,128)} fusion(bf16[1024,3584]{1,0:T(8,128)(2,1)} %constant_dynamic-update-slice_fusion, s32[]{:T(128)S(6)} %select_n.22, f32[512,768]{1,0:T(8,128)S(1)} %get-tuple-element.7, s32[512]{0:T(512)S(1)} %bitcast.12, f32[512]{0:T(512)S(1)} %get-tuple-element.5, f32[512]{0:T(512)S(1)} %bitcast.8), kind=kOutput, calls=%fused_computation | convolution fusion | flops 2822504448 | bytes 16259076 | tf_op jit(solution)/shard_map/dot_general | solution.py:57
  134.0 0.0 reduce-scatter.3.cloned.1.call-update
  134.0 0.6 multiply_reduce_fusion
  134.6 20.6 %psum.23 = f32[]{:T(128)} all-reduce(f32[]{:T(128)} %multiply_reduce_fusion), channel_id=1, replica_groups=mesh['batch'=8,'vocab'=4] {'batch'}, use_global_device_ids=true, to_apply=%region_7.8 | all-reduce | flops 1 | bytes 8 | tf_op jit(solution)/shard_map/psum | solution.py:73
  155.9 31.6 %reduce-scatter.5.cloned.1.call-done = f32[128,3584]{1,0:T(8,128)} async-done(((f32[512,3584]{1,0:T(8,128)}), f32[128,3584]{1,0:T(8,128)}) %reduce-scatter.5.cloned.1.call-update) | async-done | bytes 1835024 | tf_op jit(solution)/shard_map/reduce_scatter | solution.py:70
  187.5 190.2 %reduce-scatter.3.cloned.1.call-done = f32[448,768]{1,0:T(8,128)} async-done(((f32[3584,768]{1,0:T(8,128)}), f32[448,768]{1,0:T(8,128)}) %reduce-scatter.3.cloned.1.call-update) | async-done | bytes 1376272 | tf_op jit(solution)/shard_map/reduce_scatter | solution.py:56
  (2 shorter events, 0.0 us)
Async XLA Ops:
  7.2 94.9 %all-gather.4.cloned.1.call-start = ((), (), s32[]{:S(2)}) async-start(), calls=%async_computation.2 | async-start | bytes 6193152 | tf_op jit(solution)/shard_map/all_gather | solution.py:41
  7.9 179.6 %reduce-scatter.5.cloned.1.call-start = ((), (), s32[]{:S(2)}) async-start(), calls=%async_computation.4 | async-start | bytes 9175040 | tf_op jit(solution)/shard_map/reduce_scatter | solution.py:70
  7.9 13.7 %collective-permute-start = (bf16[128,3584]{1,0:T(8,128)(2,1)}, bf16[128,3584]{1,0:T(8,128)(2,1)S(1)}, u32[]{:S(2)}, u32[]{:S(2)}) collective-permute-start(bf16[128,3584]{1,0:T(8,128)(2,1)} %param.4), channel_id=1, source_target_pairs={{0,1},{1,2},{2,3},{3,0},{4,5},{5,6},{6,7},{7,4},{8,9},{9,10},{10,1... | collective-permute-start | bytes 2752520 | tf_op jit(solution)/shard_map/ppermute | solution.py:13
  21.7 12.8 %collective-permute-start.1 = (bf16[128,3584]{1,0:T(8,128)(2,1)S(1)}, bf16[128,3584]{1,0:T(8,128)(2,1)S(1)}, u32[]{:S(2)}, u32[]{:S(2)}) collective-permute-start(bf16[128,3584]{1,0:T(8,128)(2,1)S(1)} %collective-permute-done), channel_id=1, source_target_pairs={{0,1},{1,2},{2,3},{3,0},{4,5},{5,6},{6,7},{7,4},{8,9},{9,10},{10,1... | collective-permute-start | bytes 2752520 | tf_op jit(solution)/shard_map/ppermute | solution.py:13
  34.5 19.2 %collective-permute-start.2 = (bf16[128,3584]{1,0:T(8,128)(2,1)S(1)}, bf16[128,3584]{1,0:T(8,128)(2,1)S(1)}, u32[]{:S(2)}, u32[]{:S(2)}) collective-permute-start(bf16[128,3584]{1,0:T(8,128)(2,1)S(1)} %collective-permute-done.1), channel_id=1, source_target_pairs={{0,1},{1,2},{2,3},{3,0},{4,5},{5,6},{6,7},{7,4},{8,9},{9,10},{10,1... | collective-permute-start | bytes 2752520 | tf_op jit(solution)/shard_map/ppermute | solution.py:13
  54.7 2.0 copy-start
  122.9 254.7 %reduce-scatter.3.cloned.1.call-start = ((), (), s32[]{:S(2)}) async-start(), calls=%async_computation.3 | async-start | bytes 12386304 | tf_op jit(solution)/shard_map/reduce_scatter | solution.py:56
Sparse Core Ops, SparseCore 0:
  10.2 91.8 all-gather.3
  123.1 64.3 reduce-scatter.4
  191.7 185.9 reduce-scatter.2
